TPU v7x, 128 devices: a whole 4x4x4 slice. The times are simulated.
128 devices in a mesh: tm: 2 (over z_lo), grid: 64 (over z_hi, y, x, core).
Axes of the slice: x: 4, y: 4, z: 4 (z_hi: 2, z_lo: 2; z = z_hi * 2 + z_lo), core: 2. Of those that a mesh axis runs over, the one named last changes fastest.
Arguments:
- occupied_green: bfloat16 [2, 1024, 1024], P('tm', 'grid'), may hold values from -0.005859375 to 0.005859375
- empty_green: bfloat16 [2, 1024, 1024], P('tm', 'grid'), may hold values from -0.005859375 to 0.005859375
- basis: bfloat16 [12288, 1024], P('grid'), may hold values from -8 to 8
- time_weights: float32 [2, 2], replicated, may hold values from 0.25 to 1
Outputs:
- polarizability: float32 [2, 1024, 1024], P('tm', 'grid')
All inputs are finite; a program needn't handle non-finite values.
Results may differ from a plain program's by a relative error of at most 0.0012.
Values may be sent and summed in bfloat16 or wider, within the bound.
No kernel may reach another device: no remote copies, remote signals or barrier semaphores. Data moves between devices by JAX's collectives and lax.ppermute only.
A program may use at most 128 MiB of HBM per device.

v0:
```python
import jax
import jax.numpy as jnp
from jax import lax
from jax.sharding import Mesh
from jax.sharding import PartitionSpec as P

NR = 12288
NB = 1024
GRID = ("grid_0", "grid_1", "grid_2", "grid_3")


def cut_along(x, dim, devices):
    shape = x.shape
    tiles = x.reshape(*shape[:dim], devices, shape[dim] // devices, *shape[dim + 1 :])
    return jnp.moveaxis(tiles, dim, 0)


def laid_out(tiles, dim):
    shape = list(tiles.shape[1:])
    shape[dim] *= tiles.shape[0]
    return jnp.moveaxis(tiles, 0, dim).reshape(shape)


def moved_by_axis(tiles, axes, order):
    shape = [lax.axis_size(a) for a in axes]
    tiles = tiles.reshape(*shape, *tiles.shape[1:])
    for k in order:
        tiles = lax.all_to_all(tiles, axes[k], split_axis=k, concat_axis=k, tiled=True)
    return tiles.reshape(-1, *tiles.shape[len(axes) :])


def two_step_exchange(x, groups, order, split_dim, concat_dim):
    devices = lax.axis_size(groups[0]) * lax.axis_size(groups[1])
    tiles = cut_along(x, split_dim, devices)
    return laid_out(moved_by_axis(tiles, groups, order), concat_dim)


def sent_and_summed(x, axis, dim):
    tiles = cut_along(x, dim, lax.axis_size(axis))
    arrived = lax.all_to_all(tiles, axis, split_axis=0, concat_axis=0, tiled=True)
    return arrived.sum(axis=0)


def weigh_times(time_weights, block_list, scale_factor):
    time_count = len(block_list)
    group_index = lax.axis_index("tm")
    weights_local = lax.dynamic_slice_in_dim(time_weights, group_index * time_count, time_count, 1)
    accum = weights_local[:, 0, None, None] * block_list[0][None]
    return scale_factor * accum


def step_size(piece_rows):
    return max((divisor for divisor in range(1, 2049) if piece_rows % divisor == 0))


def shards(occupied_green, empty_green, basis, time_weights):
    stacked = jnp.stack([occupied_green, empty_green])
    time_count = occupied_green.shape[0]
    row_total = basis.shape[0]
    scale_factor = 1.0 / NR

    def make_accumulate(combined_rows):

        def accumulate(running, basis_piece, first_row):
            piece_rows = basis_piece.shape[0]
            step_rows = step_size(piece_rows)

            def one_step(step_index, inner):
                basis_subpart = lax.dynamic_slice_in_dim(
                    basis_piece, step_index * step_rows, step_rows, 0
                )
                real_pair = jnp.einsum(
                    "qoa,ba->qob", combined_rows, basis_subpart, preferred_element_type=jnp.float32
                )
                product = (real_pair[0] * real_pair[1]).astype(jnp.bfloat16)
                return inner + jnp.dot(product, basis_subpart, preferred_element_type=jnp.float32)

            return lax.fori_loop(0, piece_rows // step_rows, one_step, running)

        return accumulate

    initial = jnp.zeros((time_count * row_total, NB), jnp.float32)
    projected = jnp.einsum(
        "sl,ftkl->ftsk",
        basis,
        lax.all_gather(stacked, GRID, axis=2, tiled=True),
        preferred_element_type=jnp.float32,
    ).astype(jnp.bfloat16)
    combined_rows = projected.reshape(2, time_count * row_total, NB)
    accumulate = make_accumulate(combined_rows)
    summed = accumulate(initial, lax.all_gather(basis, GRID, axis=0, tiled=True), jnp.int32(0))
    back_half = summed.astype(jnp.bfloat16).reshape(time_count, row_total, NB)
    columns = two_step_exchange(back_half, (("grid_0", "grid_1", "grid_2"), "grid_3"), (1, 0), 2, 1)
    coef_cols = jnp.einsum(
        "tsk,sl->tkl",
        columns,
        lax.all_gather(basis, GRID, axis=0, tiled=True),
        preferred_element_type=jnp.float32,
    )
    block_list = [coef_cols[0]]
    result = sent_and_summed(weigh_times(time_weights, block_list, scale_factor), "tm", 0)
    return result


def solution(mesh):
    split = Mesh(
        mesh.devices.reshape(mesh.shape["tm"], 2, 4, 4, 2),
        ("tm", "grid_0", "grid_1", "grid_2", "grid_3"),
    )
    in_specs = (P("tm", GRID, None), P("tm", GRID, None), P(GRID, None), P())
    out_specs = P("tm", GRID, None)
    return jax.shard_map(
        shards, mesh=split, in_specs=in_specs, out_specs=out_specs, check_vma=False
    )
```

profile of v0, /device:TPU:0, one launch (start us, length us, event | category | flops | bytes accessed | tf_op | source)
XLA Modules:
  0.0 312.2 jit_solution(397094787537150573)
XLA Ops:
  6.5 1.4 pad_maximum_fusion
  8.0 0.7 all-gather.3.cloned.1.call-update
  8.7 77.5 %all-gather.5.cloned.1.call-done = bf16[2,1,1024,1024]{3,2,0,1:T(8,128)(2,1)} async-done(((bf16[2,1,16,1024]{3,2,0,1:T(8,128)(2,1)}), bf16[2,1,1024,1024]{3,2,0,1:T(8,128)(2,1)}) %all-gather.5.cloned.1.call-update) | async-done | bytes 4194320 | tf_op jit(solution)/shard_map/all_gather | solution.py:86
  86.2 3.8 %fusion.21 = bf16[2,192,1024]{2,1,0:T(8,128)(2,1)S(1)} fusion(bf16[2,1,1024,1024]{3,2,0,1:T(8,128)(2,1)} %all-gather.5.cloned.1.call-done, bf16[192,1024]{1,0:T(8,128)(2,1)} %param.8), kind=kOutput, calls=%fused_computation.15 | convolution fusion | flops 805699584 | bytes 5373952 | tf_op jit(solution)/shard_map/sl,ftkl->ftsk/dot_general | solution.py:83
  90.0 127.6 %all-gather.3.cloned.1.call-done = bf16[12288,1024]{1,0:T(8,128)(2,1)} async-done(((bf16[192,1024]{1,0:T(8,128)(2,1)}), bf16[12288,1024]{1,0:T(8,128)(2,1)}) %all-gather.3.cloned.1.call-update) | async-done | bytes 25165840 | tf_op jit(solution)/shard_map/all_gather | solution.py:91
  217.6 44.7 %while.14 = (s32[]{:T(128)}, f32[192,1024]{1,0:T(8,128)S(1)}, bf16[12288,1024]{1,0:T(8,128)(2,1)}, bf16[2,192,1024]{2,1,0:T(8,128)(2,1)S(1)}, s32[]{:T(128)}, /*index=5*/s32[]{:T(128)}, s32[]{:T(128)}, s32[]{:T(128)}) while((s32[]{:T(128)}, f32[192,1024]{1,0:T(8,128)S(1)}, bf16[12288,1024]{1,0:T(8,128)(2,1)}, ...), condition=%wide.region_1.0_spmd.clone, body=%wide.region_0.0_spmd.clone.sunk | while | flops 2417098752 | bytes 17039516 | solution.py:78
  217.6 4.0 %fusion.39 = f32[2,192,2048]{2,1,0:T(8,128)S(1)} fusion(bf16[2,192,1024]{2,1,0:T(8,128)(2,1)S(1)} %get-tuple-element.152, bf16[12288,1024]{1,0:T(8,128)(2,1)} %get-tuple-element.151, s32[]{:T(128)S(6)} %select_n.13), kind=kOutput, calls=%fused_computation.5.clone.1 | convolution fusion | flops 1610612736 | bytes 8126468 | tf_op jit(solution)/shard_map/while/body/eval_jaxpr/qoa,ba->qob/dot_general | solution.py:72
  221.6 3.4 %fusion.40 = f32[192,1024]{1,0:T(8,128)S(1)} fusion(bf16[12288,1024]{1,0:T(8,128)(2,1)} %get-tuple-element.151, s32[]{:T(128)S(6)} %select_n.13, f32[2,192,2048]{2,1,0:T(8,128)S(1)} %fusion.39, f32[192,1024]{1,0:T(8,128)S(1)} %get-tuple-element.142, pred[]{:T(512)S(6)} %compare.3), kind=kOutput, calls=%fused_computation.8.clone.1 | convolution fusion | flops 806486016 | bytes 8912901 | tf_op jit(solution)/shard_map/while/body/eval_jaxpr/dot_general | solution.py:76
  225.0 4.0 %fusion.39 = f32[2,192,2048]{2,1,0:T(8,128)S(1)} fusion(bf16[2,192,1024]{2,1,0:T(8,128)(2,1)S(1)} %get-tuple-element.152, bf16[12288,1024]{1,0:T(8,128)(2,1)} %get-tuple-element.151, s32[]{:T(128)S(6)} %select_n.13), kind=kOutput, calls=%fused_computation.5.clone.1 | convolution fusion | flops 1610612736 | bytes 8126468 | tf_op jit(solution)/shard_map/while/body/eval_jaxpr/qoa,ba->qob/dot_general | solution.py:72
  229.0 3.4 %fusion.40 = f32[192,1024]{1,0:T(8,128)S(1)} fusion(bf16[12288,1024]{1,0:T(8,128)(2,1)} %get-tuple-element.151, s32[]{:T(128)S(6)} %select_n.13, f32[2,192,2048]{2,1,0:T(8,128)S(1)} %fusion.39, f32[192,1024]{1,0:T(8,128)S(1)} %get-tuple-element.142, pred[]{:T(512)S(6)} %compare.3), kind=kOutput, calls=%fused_computation.8.clone.1 | convolution fusion | flops 806486016 | bytes 8912901 | tf_op jit(solution)/shard_map/while/body/eval_jaxpr/dot_general | solution.py:76
  232.5 4.0 %fusion.39 = f32[2,192,2048]{2,1,0:T(8,128)S(1)} fusion(bf16[2,192,1024]{2,1,0:T(8,128)(2,1)S(1)} %get-tuple-element.152, bf16[12288,1024]{1,0:T(8,128)(2,1)} %get-tuple-element.151, s32[]{:T(128)S(6)} %select_n.13), kind=kOutput, calls=%fused_computation.5.clone.1 | convolution fusion | flops 1610612736 | bytes 8126468 | tf_op jit(solution)/shard_map/while/body/eval_jaxpr/qoa,ba->qob/dot_general | solution.py:72
  236.5 3.4 %fusion.40 = f32[192,1024]{1,0:T(8,128)S(1)} fusion(bf16[12288,1024]{1,0:T(8,128)(2,1)} %get-tuple-element.151, s32[]{:T(128)S(6)} %select_n.13, f32[2,192,2048]{2,1,0:T(8,128)S(1)} %fusion.39, f32[192,1024]{1,0:T(8,128)S(1)} %get-tuple-element.142, pred[]{:T(512)S(6)} %compare.3), kind=kOutput, calls=%fused_computation.8.clone.1 | convolution fusion | flops 806486016 | bytes 8912901 | tf_op jit(solution)/shard_map/while/body/eval_jaxpr/dot_general | solution.py:76
  239.9 4.0 %fusion.39 = f32[2,192,2048]{2,1,0:T(8,128)S(1)} fusion(bf16[2,192,1024]{2,1,0:T(8,128)(2,1)S(1)} %get-tuple-element.152, bf16[12288,1024]{1,0:T(8,128)(2,1)} %get-tuple-element.151, s32[]{:T(128)S(6)} %select_n.13), kind=kOutput, calls=%fused_computation.5.clone.1 | convolution fusion | flops 1610612736 | bytes 8126468 | tf_op jit(solution)/shard_map/while/body/eval_jaxpr/qoa,ba->qob/dot_general | solution.py:72
  243.9 3.4 %fusion.40 = f32[192,1024]{1,0:T(8,128)S(1)} fusion(bf16[12288,1024]{1,0:T(8,128)(2,1)} %get-tuple-element.151, s32[]{:T(128)S(6)} %select_n.13, f32[2,192,2048]{2,1,0:T(8,128)S(1)} %fusion.39, f32[192,1024]{1,0:T(8,128)S(1)} %get-tuple-element.142, pred[]{:T(512)S(6)} %compare.3), kind=kOutput, calls=%fused_computation.8.clone.1 | convolution fusion | flops 806486016 | bytes 8912901 | tf_op jit(solution)/shard_map/while/body/eval_jaxpr/dot_general | solution.py:76
  247.4 4.0 %fusion.39 = f32[2,192,2048]{2,1,0:T(8,128)S(1)} fusion(bf16[2,192,1024]{2,1,0:T(8,128)(2,1)S(1)} %get-tuple-element.152, bf16[12288,1024]{1,0:T(8,128)(2,1)} %get-tuple-element.151, s32[]{:T(128)S(6)} %select_n.13), kind=kOutput, calls=%fused_computation.5.clone.1 | convolution fusion | flops 1610612736 | bytes 8126468 | tf_op jit(solution)/shard_map/while/body/eval_jaxpr/qoa,ba->qob/dot_general | solution.py:72
  251.4 3.4 %fusion.40 = f32[192,1024]{1,0:T(8,128)S(1)} fusion(bf16[12288,1024]{1,0:T(8,128)(2,1)} %get-tuple-element.151, s32[]{:T(128)S(6)} %select_n.13, f32[2,192,2048]{2,1,0:T(8,128)S(1)} %fusion.39, f32[192,1024]{1,0:T(8,128)S(1)} %get-tuple-element.142, pred[]{:T(512)S(6)} %compare.3), kind=kOutput, calls=%fused_computation.8.clone.1 | convolution fusion | flops 806486016 | bytes 8912901 | tf_op jit(solution)/shard_map/while/body/eval_jaxpr/dot_general | solution.py:76
  254.8 4.0 %fusion.39 = f32[2,192,2048]{2,1,0:T(8,128)S(1)} fusion(bf16[2,192,1024]{2,1,0:T(8,128)(2,1)S(1)} %get-tuple-element.152, bf16[12288,1024]{1,0:T(8,128)(2,1)} %get-tuple-element.151, s32[]{:T(128)S(6)} %select_n.13), kind=kOutput, calls=%fused_computation.5.clone.1 | convolution fusion | flops 1610612736 | bytes 8126468 | tf_op jit(solution)/shard_map/while/body/eval_jaxpr/qoa,ba->qob/dot_general | solution.py:72
  258.8 3.4 %fusion.40 = f32[192,1024]{1,0:T(8,128)S(1)} fusion(bf16[12288,1024]{1,0:T(8,128)(2,1)} %get-tuple-element.151, s32[]{:T(128)S(6)} %select_n.13, f32[2,192,2048]{2,1,0:T(8,128)S(1)} %fusion.39, f32[192,1024]{1,0:T(8,128)S(1)} %get-tuple-element.142, pred[]{:T(512)S(6)} %compare.3), kind=kOutput, calls=%fused_computation.8.clone.1 | convolution fusion | flops 806486016 | bytes 8912901 | tf_op jit(solution)/shard_map/while/body/eval_jaxpr/dot_general | solution.py:76
  262.8 4.2 %all_to_all.15 = bf16[32,2,1,192,16]{3,0,4,2,1:T(8,128)(2,1)S(1)} all-to-all(bf16[32,2,1,192,16]{3,0,4,2,1:T(8,128)(2,1)S(1)} %copy.12), channel_id=1, replica_groups=mesh['tm'=2,'grid_0'=2,'grid_1'=4,'grid_2'=4,'grid_3'=2] {'grid_3'}, dimensions={1} | all-to-all | bytes 786432 | tf_op jit(solution)/shard_map/all_to_all | solution.py:28
  266.9 1.4 copy.13
  268.3 5.4 %all-to-all-start.1 = ((bf16[32,2,1,192,16]{3,1,4,2,0:T(2,128)(2,1)}), bf16[32,2,1,192,16]{3,1,4,2,0:T(2,128)(2,1)S(1)}, u32[]{:S(2)}, u32[]{:S(2)}) async-start(bf16[32,2,1,192,16]{3,1,4,2,0:T(2,128)(2,1)} %copy.13), calls=%async_computation.1 | async-start | bytes 1048576 | tf_op jit(solution)/shard_map/all_to_all | solution.py:28
  273.9 12.9 %all-to-all-done.1 = bf16[32,2,1,192,16]{3,1,4,2,0:T(2,128)(2,1)S(1)} async-done(((bf16[32,2,1,192,16]{3,1,4,2,0:T(2,128)(2,1)}), bf16[32,2,1,192,16]{3,1,4,2,0:T(2,128)(2,1)S(1)}, u32[]{:S(2)}, u32[]{:S(2)}) %all-to-all-start.1) | async-done | bytes 393248 | tf_op jit(solution)/shard_map/all_to_all | solution.py:28
  287.8 9.9 %fusion.25 = f32[16,1024]{1,0:T(8,128)S(1)} fusion(bf16[12288,16]{0,1:T(8,128)(2,1)S(1)} %reshape.31, bf16[12288,1024]{1,0:T(8,128)(2,1)} %get-tuple-element.160), kind=kOutput, calls=%fused_computation.20 | convolution fusion | flops 402653184 | bytes 25624576 | tf_op jit(solution)/shard_map/tsk,sl->tkl/dot_general | solution.py:94
  297.8 6.9 %all_to_all.16 = f32[2,1,16,1024]{3,2,1,0:T(8,128)S(1)} all-to-all(f32[2,1,16,1024]{3,2,1,0:T(8,128)S(1)} %multiply_multiply_fusion), channel_id=1, replica_groups=mesh['tm'=2,'grid_0'=2,'grid_1'=4,'grid_2'=4,'grid_3'=2] {'tm'}, dimensions={0} | all-to-all | bytes 262144 | tf_op jit(solution)/shard_map/all_to_all | solution.py:40
  (13 shorter events, 2.5 us)
Async XLA Ops:
  6.5 267.2 %copy-start = (f32[2,2]{1,0:T(2,128)S(1)}, f32[2,2]{1,0:T(2,128)}, u32[]{:S(2)}) copy-start(f32[2,2]{1,0:T(2,128)} %param.9) | copy-start | bytes 52
  6.5 79.7 %all-gather.5.cloned.1.call-start = ((), (), s32[]{:S(2)}) async-start(), calls=%async_computation.4 | async-start | bytes 4259840 | tf_op jit(solution)/shard_map/all_gather | solution.py:86
  8.0 209.6 %all-gather.3.cloned.1.call-start = ((), (), s32[]{:S(2)}) async-start(), calls=%async_computation.3 | async-start | bytes 25559040 | tf_op jit(solution)/shard_map/all_gather | solution.py:91
  268.3 18.5 %all-to-all-start.1 = ((bf16[32,2,1,192,16]{3,1,4,2,0:T(2,128)(2,1)}), bf16[32,2,1,192,16]{3,1,4,2,0:T(2,128)(2,1)S(1)}, u32[]{:S(2)}, u32[]{:S(2)}) async-start(bf16[32,2,1,192,16]{3,1,4,2,0:T(2,128)(2,1)} %copy.13), calls=%async_computation.1 | async-start | bytes 1048576 | tf_op jit(solution)/shard_map/all_to_all | solution.py:28
Sparse Core Ops, SparseCore 0:
  10.6 75.5 all-gather.4
  89.5 128.0 all-gather.2
where the time goes:
time: 313 us; the launch traced here: 312 us
  waiting for transfers between devices  219 us (70%)
  matrix products  58.1 us (19%)
  between operations  13.5 us (4%)
  blocking collectives  11.1 us (4%)
  starting transfers between devices  5.47 us (2%)
    all_gather x1, waiting for transfers between devices, shards(): lax.all_gather(basis, GRID, axis=0, tiled=True)  128 us
    all_gather x1, waiting for transfers between devices, shards(): lax.all_gather(stacked, GRID, axis=2, tiled=True)  77.5 us
    dot_general x6, matrix products, one_step(): jnp.einsum('qoa,ba->qob', combined_rows, basis_subpart, preferred_element...  24.1 us
    dot_general x6, matrix products, one_step(): jnp.dot(product, basis_subpart, preferred_element_type=jnp.float32)  20.4 us
    all_to_all x1, waiting for transfers between devices, moved_by_axis(): lax.all_to_all(tiles, axes[k], split_axis=k, concat_axis=k, tiled=True)  12.9 us
    dot_general x1, matrix products, shards(): jnp.einsum('tsk,sl->tkl', columns, lax.all_gather(basis, GRID, axis=0, ti...  9.89 us
    all_to_all x1, blocking collectives, sent_and_summed(): lax.all_to_all(tiles, axis, split_axis=0, concat_axis=0, tiled=True)  6.9 us
  transfers between devices with their start and end apart: 3, of which 3 were waited for; matrix products, arithmetic and copies ran while one was open for 1% of the time, Pallas kernels for 0%

commit v1 on v0

--- a/solution.py
+++ b/solution.py
@@ -7,6 +7,11 @@
 NR = 12288
 NB = 1024
 GRID = ("grid_0", "grid_1", "grid_2", "grid_3")
+
+
+def all_by_exchange(x, axis, along):
+    repeated = jnp.stack([x] * lax.axis_size(axis))
+    return jnp.concatenate(lax.all_to_all(repeated, axis, 0, 0), axis=along)
 
 
 def cut_along(x, dim, devices):
@@ -83,7 +88,7 @@
     projected = jnp.einsum(
         "sl,ftkl->ftsk",
         basis,
-        lax.all_gather(stacked, GRID, axis=2, tiled=True),
+        all_by_exchange(stacked, GRID, 2),
         preferred_element_type=jnp.float32,
     ).astype(jnp.bfloat16)
     combined_rows = projected.reshape(2, time_count * row_total, NB)

time: 313 us -> 298 us (0.952)
  waiting for transfers between devices: 219 us -> 174 us
  matrix products: 58.1 us -> 71.6 us
  starting transfers between devices: 5.47 us -> 17 us
  local copies, waits for them, and re-layouts: 3.09 us -> 8.24 us
    all_gather x1 -> x0, waiting for transfers between devices: 77.5 us -> none  [shards(): lax.all_gather(stacked, GRID, axis=2, tiled=True)]
    all_to_all x0 -> x1, waiting for transfers between devices: none -> 56.1 us  [all_by_exchange(): return jnp.concatenate(lax.all_to_all(repeated, axis, 0, 0), axis=along)]
    all_gather x1, waiting for transfers between devices: 128 us -> 104 us  [shards(): lax.all_gather(basis, GRID, axis=0, tiled=True)]
    all_to_all x0 -> x1, starting transfers between devices: none -> 11.6 us  [all_by_exchange(): return jnp.concatenate(lax.all_to_all(repeated, axis, 0, 0), axis=along)]
    dot_general x6, matrix products: 24.1 us -> 34.5 us  [one_step(): jnp.einsum('qoa,ba->qob', combined_rows, basis_subpart, preferred_element...]
    dot_general x6, matrix products: 20.4 us -> 25.7 us  [one_step(): jnp.dot(product, basis_subpart, preferred_element_type=jnp.float32)]
  transfers between devices with their start and end apart: 3 -> 3, of which waited for: 3 -> 3; matrix products, arithmetic and copies ran while one was open for 1% -> 3% of each run, Pallas kernels for 0% -> 0%
where the time goes in v1:
time: 298 us; the launch traced here: 297 us
  waiting for transfers between devices  174 us (58%)
  matrix products  71.6 us (24%)
  starting transfers between devices  17 us (6%)
  between operations  13.5 us (5%)
  blocking collectives  11.1 us (4%)
  local copies, waits for them, and re-layouts  8.24 us (3%)
    all_gather x1, waiting for transfers between devices, shards(): lax.all_gather(basis, GRID, axis=0, tiled=True)  104 us
    all_to_all x1, waiting for transfers between devices, all_by_exchange(): return jnp.concatenate(lax.all_to_all(repeated, axis, 0, 0), axis=along)  56.1 us
    dot_general x6, matrix products, one_step(): jnp.einsum('qoa,ba->qob', combined_rows, basis_subpart, preferred_element...  34.5 us
    dot_general x6, matrix products, one_step(): jnp.dot(product, basis_subpart, preferred_element_type=jnp.float32)  25.7 us
    all_to_all x1, waiting for transfers between devices, moved_by_axis(): lax.all_to_all(tiles, axes[k], split_axis=k, concat_axis=k, tiled=True)  12.9 us
    all_to_all x1, starting transfers between devices, all_by_exchange(): return jnp.concatenate(lax.all_to_all(repeated, axis, 0, 0), axis=along)  11.6 us
    dot_general x1, matrix products, shards(): jnp.einsum('tsk,sl->tkl', columns, lax.all_gather(basis, GRID, axis=0, ti...  9.89 us
    all_to_all x1, blocking collectives, sent_and_summed(): lax.all_to_all(tiles, axis, split_axis=0, concat_axis=0, tiled=True)  6.91 us
  transfers between devices with their start and end apart: 3, of which 3 were waited for; matrix products, arithmetic and copies ran while one was open for 3% of the time, Pallas kernels for 0%

profile of v1, /device:TPU:0, one launch (start us, length us, event | category | flops | bytes accessed | tf_op | source)
XLA Modules:
  0.0 297.3 jit_solution(16287569648246031915)
XLA Ops:
  8.0 2.5 stack.14
  10.5 11.6 %all-to-all-start = ((bf16[64,2,1,16,1024]{4,3,1,2,0:T(8,128)(2,1)}), bf16[64,2,1,16,1024]{4,3,1,2,0:T(8,128)(2,1)}, u32[]{:S(2)}, u32[]{:S(2)}) async-start(bf16[64,2,1,16,1024]{4,3,1,2,0:T(8,128)(2,1)} %stack.14), calls=%async_computation | async-start | bytes 8388608 | tf_op jit(solution)/shard_map/all_to_all | solution.py:14
  22.2 56.1 %all-to-all-done = bf16[64,2,1,16,1024]{4,3,1,2,0:T(8,128)(2,1)} async-done(((bf16[64,2,1,16,1024]{4,3,1,2,0:T(8,128)(2,1)}), bf16[64,2,1,16,1024]{4,3,1,2,0:T(8,128)(2,1)}, u32[]{:S(2)}, u32[]{:S(2)}) %all-to-all-start) | async-done | bytes 4194336 | tf_op jit(solution)/shard_map/all_to_all | solution.py:14
  78.3 2.7 copy.12
  81.0 1.5 fusion.16
  82.5 104.5 %all-gather.2.cloned.1.call-done = bf16[12288,1024]{1,0:T(8,128)(2,1)} async-done(((bf16[192,1024]{1,0:T(8,128)(2,1)}), bf16[12288,1024]{1,0:T(8,128)(2,1)}) %all-gather.2.cloned.1.call-update) | async-done | bytes 25165840 | tf_op jit(solution)/shard_map/all_gather | solution.py:96
  187.0 60.4 %while.14 = (s32[]{:T(128)}, f32[192,1024]{1,0:T(8,128)S(1)}, bf16[12288,1024]{1,0:T(8,128)(2,1)}, bf16[2,192,1024]{2,1,0:T(8,128)(2,1)S(1)}, s32[]{:T(128)}, /*index=5*/s32[]{:T(128)}, s32[]{:T(128)}, s32[]{:T(128)}) while((s32[]{:T(128)}, f32[192,1024]{1,0:T(8,128)S(1)}, bf16[12288,1024]{1,0:T(8,128)(2,1)}, ...), condition=%wide.region_1.0_spmd.clone, body=%wide.region_0.0_spmd.clone.sunk | while | flops 2417098752 | bytes 17039508 | solution.py:83
  187.0 5.7 %fusion.33 = f32[2,192,2048]{2,1,0:T(8,128)} fusion(bf16[2,192,1024]{2,1,0:T(8,128)(2,1)S(1)} %get-tuple-element.152, bf16[12288,1024]{1,0:T(8,128)(2,1)} %get-tuple-element.151, s32[]{:T(128)S(6)} %select_n.13), kind=kOutput, calls=%fused_computation.5.clone.1 | convolution fusion | flops 1610612736 | bytes 8126468 | tf_op jit(solution)/shard_map/while/body/eval_jaxpr/qoa,ba->qob/dot_general | solution.py:77
  192.8 4.3 %fusion.34 = f32[192,1024]{1,0:T(8,128)S(1)} fusion(bf16[12288,1024]{1,0:T(8,128)(2,1)} %get-tuple-element.151, s32[]{:T(128)S(6)} %select_n.13, f32[2,192,2048]{2,1,0:T(8,128)} %fusion.33, f32[192,1024]{1,0:T(8,128)S(1)} %get-tuple-element.142, pred[]{:T(512)S(6)} %compare.3), kind=kOutput, calls=%fused_computation.8.clone.1 | convolution fusion | flops 806486016 | bytes 8912901 | tf_op jit(solution)/shard_map/while/body/eval_jaxpr/dot_general | solution.py:81
  197.1 5.7 %fusion.33 = f32[2,192,2048]{2,1,0:T(8,128)} fusion(bf16[2,192,1024]{2,1,0:T(8,128)(2,1)S(1)} %get-tuple-element.152, bf16[12288,1024]{1,0:T(8,128)(2,1)} %get-tuple-element.151, s32[]{:T(128)S(6)} %select_n.13), kind=kOutput, calls=%fused_computation.5.clone.1 | convolution fusion | flops 1610612736 | bytes 8126468 | tf_op jit(solution)/shard_map/while/body/eval_jaxpr/qoa,ba->qob/dot_general | solution.py:77
  202.8 4.3 %fusion.34 = f32[192,1024]{1,0:T(8,128)S(1)} fusion(bf16[12288,1024]{1,0:T(8,128)(2,1)} %get-tuple-element.151, s32[]{:T(128)S(6)} %select_n.13, f32[2,192,2048]{2,1,0:T(8,128)} %fusion.33, f32[192,1024]{1,0:T(8,128)S(1)} %get-tuple-element.142, pred[]{:T(512)S(6)} %compare.3), kind=kOutput, calls=%fused_computation.8.clone.1 | convolution fusion | flops 806486016 | bytes 8912901 | tf_op jit(solution)/shard_map/while/body/eval_jaxpr/dot_general | solution.py:81
  207.1 5.7 %fusion.33 = f32[2,192,2048]{2,1,0:T(8,128)} fusion(bf16[2,192,1024]{2,1,0:T(8,128)(2,1)S(1)} %get-tuple-element.152, bf16[12288,1024]{1,0:T(8,128)(2,1)} %get-tuple-element.151, s32[]{:T(128)S(6)} %select_n.13), kind=kOutput, calls=%fused_computation.5.clone.1 | convolution fusion | flops 1610612736 | bytes 8126468 | tf_op jit(solution)/shard_map/while/body/eval_jaxpr/qoa,ba->qob/dot_general | solution.py:77
  212.9 4.3 %fusion.34 = f32[192,1024]{1,0:T(8,128)S(1)} fusion(bf16[12288,1024]{1,0:T(8,128)(2,1)} %get-tuple-element.151, s32[]{:T(128)S(6)} %select_n.13, f32[2,192,2048]{2,1,0:T(8,128)} %fusion.33, f32[192,1024]{1,0:T(8,128)S(1)} %get-tuple-element.142, pred[]{:T(512)S(6)} %compare.3), kind=kOutput, calls=%fused_computation.8.clone.1 | convolution fusion | flops 806486016 | bytes 8912901 | tf_op jit(solution)/shard_map/while/body/eval_jaxpr/dot_general | solution.py:81
  217.2 5.7 %fusion.33 = f32[2,192,2048]{2,1,0:T(8,128)} fusion(bf16[2,192,1024]{2,1,0:T(8,128)(2,1)S(1)} %get-tuple-element.152, bf16[12288,1024]{1,0:T(8,128)(2,1)} %get-tuple-element.151, s32[]{:T(128)S(6)} %select_n.13), kind=kOutput, calls=%fused_computation.5.clone.1 | convolution fusion | flops 1610612736 | bytes 8126468 | tf_op jit(solution)/shard_map/while/body/eval_jaxpr/qoa,ba->qob/dot_general | solution.py:77
  222.9 4.3 %fusion.34 = f32[192,1024]{1,0:T(8,128)S(1)} fusion(bf16[12288,1024]{1,0:T(8,128)(2,1)} %get-tuple-element.151, s32[]{:T(128)S(6)} %select_n.13, f32[2,192,2048]{2,1,0:T(8,128)} %fusion.33, f32[192,1024]{1,0:T(8,128)S(1)} %get-tuple-element.142, pred[]{:T(512)S(6)} %compare.3), kind=kOutput, calls=%fused_computation.8.clone.1 | convolution fusion | flops 806486016 | bytes 8912901 | tf_op jit(solution)/shard_map/while/body/eval_jaxpr/dot_general | solution.py:81
  227.3 5.7 %fusion.33 = f32[2,192,2048]{2,1,0:T(8,128)} fusion(bf16[2,192,1024]{2,1,0:T(8,128)(2,1)S(1)} %get-tuple-element.152, bf16[12288,1024]{1,0:T(8,128)(2,1)} %get-tuple-element.151, s32[]{:T(128)S(6)} %select_n.13), kind=kOutput, calls=%fused_computation.5.clone.1 | convolution fusion | flops 1610612736 | bytes 8126468 | tf_op jit(solution)/shard_map/while/body/eval_jaxpr/qoa,ba->qob/dot_general | solution.py:77
  233.0 4.3 %fusion.34 = f32[192,1024]{1,0:T(8,128)S(1)} fusion(bf16[12288,1024]{1,0:T(8,128)(2,1)} %get-tuple-element.151, s32[]{:T(128)S(6)} %select_n.13, f32[2,192,2048]{2,1,0:T(8,128)} %fusion.33, f32[192,1024]{1,0:T(8,128)S(1)} %get-tuple-element.142, pred[]{:T(512)S(6)} %compare.3), kind=kOutput, calls=%fused_computation.8.clone.1 | convolution fusion | flops 806486016 | bytes 8912901 | tf_op jit(solution)/shard_map/while/body/eval_jaxpr/dot_general | solution.py:81
  237.3 5.7 %fusion.33 = f32[2,192,2048]{2,1,0:T(8,128)} fusion(bf16[2,192,1024]{2,1,0:T(8,128)(2,1)S(1)} %get-tuple-element.152, bf16[12288,1024]{1,0:T(8,128)(2,1)} %get-tuple-element.151, s32[]{:T(128)S(6)} %select_n.13), kind=kOutput, calls=%fused_computation.5.clone.1 | convolution fusion | flops 1610612736 | bytes 8126468 | tf_op jit(solution)/shard_map/while/body/eval_jaxpr/qoa,ba->qob/dot_general | solution.py:77
  243.1 4.3 %fusion.34 = f32[192,1024]{1,0:T(8,128)S(1)} fusion(bf16[12288,1024]{1,0:T(8,128)(2,1)} %get-tuple-element.151, s32[]{:T(128)S(6)} %select_n.13, f32[2,192,2048]{2,1,0:T(8,128)} %fusion.33, f32[192,1024]{1,0:T(8,128)S(1)} %get-tuple-element.142, pred[]{:T(512)S(6)} %compare.3), kind=kOutput, calls=%fused_computation.8.clone.1 | convolution fusion | flops 806486016 | bytes 8912901 | tf_op jit(solution)/shard_map/while/body/eval_jaxpr/dot_general | solution.py:81
  247.9 4.2 %all_to_all.20 = bf16[32,2,1,192,16]{3,0,4,2,1:T(8,128)(2,1)S(1)} all-to-all(bf16[32,2,1,192,16]{3,0,4,2,1:T(8,128)(2,1)S(1)} %copy.14), channel_id=1, replica_groups=mesh['tm'=2,'grid_0'=2,'grid_1'=4,'grid_2'=4,'grid_3'=2] {'grid_3'}, dimensions={1} | all-to-all | bytes 786432 | tf_op jit(solution)/shard_map/all_to_all | solution.py:33
  253.4 5.4 %all-to-all-start.2 = ((bf16[32,2,1,192,16]{3,1,4,2,0:T(2,128)(2,1)}), bf16[32,2,1,192,16]{3,1,4,2,0:T(2,128)(2,1)S(1)}, u32[]{:S(2)}, u32[]{:S(2)}) async-start(bf16[32,2,1,192,16]{3,1,4,2,0:T(2,128)(2,1)} %copy.15), calls=%async_computation.2 | async-start | bytes 1048576 | tf_op jit(solution)/shard_map/all_to_all | solution.py:33
  259.1 12.9 %all-to-all-done.2 = bf16[32,2,1,192,16]{3,1,4,2,0:T(2,128)(2,1)S(1)} async-done(((bf16[32,2,1,192,16]{3,1,4,2,0:T(2,128)(2,1)}), bf16[32,2,1,192,16]{3,1,4,2,0:T(2,128)(2,1)S(1)}, u32[]{:S(2)}, u32[]{:S(2)}) %all-to-all-start.2) | async-done | bytes 393248 | tf_op jit(solution)/shard_map/all_to_all | solution.py:33
  273.0 9.9 %fusion.18 = f32[16,1024]{1,0:T(8,128)S(1)} fusion(bf16[12288,16]{0,1:T(8,128)(2,1)S(1)} %reshape.40, bf16[12288,1024]{1,0:T(8,128)(2,1)} %get-tuple-element.159), kind=kOutput, calls=%fused_computation.18 | convolution fusion | flops 402653184 | bytes 25624576 | tf_op jit(solution)/shard_map/tsk,sl->tkl/dot_general | solution.py:99
  282.9 6.9 %all_to_all.21 = f32[2,1,16,1024]{3,2,1,0:T(8,128)S(1)} all-to-all(f32[2,1,16,1024]{3,2,1,0:T(8,128)S(1)} %multiply_multiply_fusion), channel_id=1, replica_groups=mesh['tm'=2,'grid_0'=2,'grid_1'=4,'grid_2'=4,'grid_3'=2] {'tm'}, dimensions={0} | all-to-all | bytes 262144 | tf_op jit(solution)/shard_map/all_to_all | solution.py:45
  (16 shorter events, 5.3 us)
Async XLA Ops:
  6.5 252.3 %copy-start = (f32[2,2]{1,0:T(2,128)S(1)}, f32[2,2]{1,0:T(2,128)}, u32[]{:S(2)}) copy-start(f32[2,2]{1,0:T(2,128)} %param.9) | copy-start | bytes 52
  6.5 180.5 %all-gather.2.cloned.1.call-start = ((), (), s32[]{:S(2)}) async-start(), calls=%async_computation.4 | async-start | bytes 25559040 | tf_op jit(solution)/shard_map/all_gather | solution.py:96
  10.5 67.8 %all-to-all-start = ((bf16[64,2,1,16,1024]{4,3,1,2,0:T(8,128)(2,1)}), bf16[64,2,1,16,1024]{4,3,1,2,0:T(8,128)(2,1)}, u32[]{:S(2)}, u32[]{:S(2)}) async-start(bf16[64,2,1,16,1024]{4,3,1,2,0:T(8,128)(2,1)} %stack.14), calls=%async_computation | async-start | bytes 8388608 | tf_op jit(solution)/shard_map/all_to_all | solution.py:14
  78.3 2.7 copy-start.1
  253.4 18.5 %all-to-all-start.2 = ((bf16[32,2,1,192,16]{3,1,4,2,0:T(2,128)(2,1)}), bf16[32,2,1,192,16]{3,1,4,2,0:T(2,128)(2,1)S(1)}, u32[]{:S(2)}, u32[]{:S(2)}) async-start(bf16[32,2,1,192,16]{3,1,4,2,0:T(2,128)(2,1)} %copy.15), calls=%async_computation.2 | async-start | bytes 1048576 | tf_op jit(solution)/shard_map/all_to_all | solution.py:33
Sparse Core Ops, SparseCore 0:
  10.6 176.3 all-gather.1
